TPU v7x, 32 devices: a whole 2x2x4 slice. The times are simulated.
32 devices in a mesh: pair: 4 (over x, core), ep: 8 (over z, y).
Axes of the slice: x: 2, y: 2, z: 4, core: 2. Of those that a mesh axis runs over, the one named last changes fastest.
Arguments:
- tokens: bfloat16 [8192, 4096], P(('pair', 'ep')), may hold values from -6 to 6
- expert_of: int32 [8192, 1], P(('pair', 'ep')), may hold values from 0 to 31, as said below
- w_gate: bfloat16 [32, 4096, 768], P(('pair', 'ep')), may hold values from -0.09375 to 0.09375
- w_up: bfloat16 [32, 4096, 768], P(('pair', 'ep')), may hold values from -0.09375 to 0.09375
- w_down: bfloat16 [32, 768, 4096], P(('pair', 'ep')), may hold values from -0.21875 to 0.21875
Outputs:
- mixed: bfloat16 [8192, 4096], P(('pair', 'ep'))
Inputs may be any that keep to these rules, and one draw needn't show every extreme that they name: `expert_of`: the rows of one device (aligned blocks of 256 tokens) name no expert more than 12 times; in every draw one expert, drawn from the seed, is named exactly 12 times in every device's rows.
All inputs are finite; a program needn't handle non-finite values.
Results may differ from a plain program's by a relative error of at most 0.005.
Values may be sent and summed in bfloat16 or wider, within the bound.
A program may use at most 128 MiB of HBM per device.

v0:
```python
import functools

import jax
import jax.numpy as jnp
from jax import lax
from jax.experimental import pallas as pl
from jax.experimental.pallas import tpu as pltpu
from jax.sharding import PartitionSpec as P

MESH = pl.DeviceIdType.MESH
TILE = 16
GROUP = 8


def dot(a, b):
    return jnp.dot(a, b, preferred_element_type=jnp.float32)


def exchange_ffn(
    pairs, eps, cap, row_keys, col_keys, tok_hbm, gate_hbm, up_hbm, down_hbm, head_ref, ends_ref,
    tok, outgoing, recv, result, returned, gate, up, down, hidden, rest,
    tok_sem, w_sem, local_sem, send1, recv1, send2, recv2,
):
    n = pairs * eps
    pair, ep = lax.axis_index("pair"), lax.axis_index("ep")
    tok_rows = tok.shape[0]
    width = recv.shape[2]
    tail = rest.shape[1]
    parts = cap // (TILE - cap)
    spare = TILE - cap
    rows = GROUP * TILE
    bf16 = jnp.bfloat16

    def shift(k):
        i = k // pairs
        de = (eps // 2 + ((i + 1) // 2) * (2 * ((i + 1) % 2) - 1) + eps) % eps
        return (k + 1) % pairs, de

    def target(k):
        dp, de = shift(k)
        return lax.rem(pair + dp, pairs), lax.rem(ep + de, eps)

    def origin(k):
        dp, de = shift(k)
        return lax.rem(pair + pairs - dp, pairs), lax.rem(ep + eps - de, eps)

    tok_load = pltpu.make_async_copy(tok_hbm, tok, tok_sem.at[0])
    tok_load.start()

    barrier = pltpu.get_barrier_semaphore()

    @pl.loop(0, n - 1)
    def _(k):
        p, e = target(k)
        pl.semaphore_signal(barrier, inc=1, device_id=(p, e), device_id_type=MESH)

    loads = [
        pltpu.make_async_copy(src.at[0], dst, w_sem.at[i])
        for i, (src, dst) in enumerate(((gate_hbm, gate), (up_hbm, up), (down_hbm, down)))
    ]
    for load in loads:
        load.start()

    def outbound(k):
        p, e = target(k)
        return pltpu.make_async_remote_copy(
            src_ref=outgoing.at[k],
            dst_ref=recv.at[k],
            send_sem=send1.at[k],
            recv_sem=recv1.at[k],
            device_id=(p, e),
            device_id_type=MESH,
        )

    def inbound(k):
        p, e = origin(k)
        return pltpu.make_async_remote_copy(
            src_ref=result.at[k],
            dst_ref=returned.at[k],
            send_sem=send2.at[k],
            recv_sem=recv2.at[k],
            device_id=(p, e),
            device_id_type=MESH,
        )

    def row_ids(first, shape, axis):
        at = lax.broadcasted_iota(jnp.int32, shape, axis)
        base = jnp.zeros(shape, jnp.int32)
        for i in range(GROUP):
            p, e = target(first + i)
            base = jnp.where(at // TILE == i, (p * eps + e) * TILE, base)
        return base + at % TILE

    def one_hot(mask):
        return mask.astype(jnp.float32).astype(bf16)

    def pack(first):
        ids = row_ids(first, (rows, tok_rows), 0)
        main = one_hot(row_keys[0:1, :] == ids)
        for j in range(parts):
            cols = pl.ds(j * tail, tail)
            ends = one_hot(row_keys[j + 1:j + 2, :] == ids)
            piece = dot(main, tok[:, cols]) + dot(ends, tok[:, width:])
            outgoing[pl.ds(first, GROUP), :, cols] = piece.astype(bf16).reshape(GROUP, TILE, tail)

    def unpack(first, start):
        ids = row_ids(first, (tok_rows, rows), 1)
        main = one_hot(col_keys[:, 0:1] == ids)
        ends = jnp.zeros((tok_rows, tail), jnp.float32)
        for j in range(parts):
            cols = pl.ds(j * tail, tail)
            piece = returned[pl.ds(first, GROUP), :, cols].reshape(rows, tail)
            head = dot(main, piece).astype(bf16)
            head_ref[:, cols] = head if start else head_ref[:, cols] + head
            ends = ends + dot(one_hot(col_keys[:, j + 1:j + 2] == ids), piece)
        ends = ends.astype(bf16)
        ends_ref[...] = ends if start else ends_ref[...] + ends

    def send(first):
        @pl.loop(0, GROUP)
        def _(i):
            @pl.when(first + i < n - 1)
            def _():
                outbound(first + i).start()

    tok_load.wait()
    pack(0)
    pl.semaphore_wait(barrier, n - 1)
    send(0)

    @pl.loop(1, n // GROUP)
    def _(g):
        pack(g * GROUP)
        send(g * GROUP)

    own = pltpu.make_async_copy(outgoing.at[n - 1], recv.at[n - 1], local_sem.at[0])
    own.start()
    for load in loads:
        load.wait()
    own.wait()

    r = lax.broadcasted_iota(jnp.int32, (rows, rows), 0)
    c = lax.broadcasted_iota(jnp.int32, (rows, rows), 1)
    same = (r // TILE) == (c // TILE)
    r, c = r % TILE, c % TILE

    def spreader(j):
        return one_hot(same & (r // spare == j) & (c == cap + r % spare))

    def folder(j):
        return one_hot(same & (r >= cap) & (c == spare * j + r - cap))

    body_row = (lax.broadcasted_iota(jnp.int32, (rows, 1), 0) % TILE) < cap
    step = 256

    @pl.loop(0, n // GROUP)
    def _(g):
        first = g * GROUP

        @pl.loop(0, GROUP)
        def _(i):
            @pl.when(first + i < n - 1)
            def _():
                outbound(first + i).wait_recv()

        block = recv.at[pl.ds(first, GROUP)]
        total = jnp.zeros((rows, tail), jnp.float32)
        for j in range(parts):
            piece = block[:, :, j * tail:(j + 1) * tail].reshape(rows, tail)
            total = total + dot(spreader(j), piece)
        rest[...] = total.astype(bf16)

        @pl.loop(0, hidden.shape[1] // step)
        def _(f):
            cols = pl.ds(pl.multiple_of(f * step, step), step)
            main = block[...].reshape(rows, width)
            g_out = dot(main, gate[:width, cols]) + dot(rest[...], gate[width:, cols])
            u_out = dot(main, up[:width, cols]) + dot(rest[...], up[width:, cols])
            hidden[:, cols] = (jax.nn.silu(g_out) * u_out).astype(bf16)

        rest[...] = dot(hidden[...], down[:, width:]).astype(bf16)
        for j in range(parts):
            cols = pl.ds(j * tail, tail)
            body = dot(hidden[...], down[:, cols])
            extra = dot(folder(j), rest[...])
            packed = jnp.where(body_row, body, extra).astype(bf16)
            result[pl.ds(first, GROUP), :, cols] = packed.reshape(GROUP, TILE, tail)

        @pl.loop(0, GROUP)
        def _(i):
            @pl.when(first + i < n - 1)
            def _():
                inbound(first + i).start()

    mine = pltpu.make_async_copy(result.at[n - 1], returned.at[n - 1], local_sem.at[1])
    mine.start()
    mine.wait()

    def collect(first):
        @pl.loop(0, GROUP)
        def _(i):
            @pl.when(first + i < n - 1)
            def _():
                inbound(first + i).wait_recv()

    collect(0)
    unpack(0, True)

    @pl.loop(1, n // GROUP)
    def _(g):
        collect(g * GROUP)
        unpack(g * GROUP, False)

    @pl.loop(0, n - 1)
    def _(k):
        outbound(k).wait_send()
        inbound(k).wait_send()


def fused(tokens, routed, slot, w_gate, w_up, w_down, pairs, eps, cap):
    n = pairs * eps
    tok_rows, depth = tokens.shape
    ff = w_gate.shape[2]
    spare = TILE - cap
    parts = cap // spare
    tail = depth * spare // TILE
    width = depth - tail

    rest_key = jnp.where(
        slot[None, :] // spare == jnp.arange(parts)[:, None],
        (routed * TILE + cap + slot % spare)[None, :],
        -1,
    )
    keys = jnp.concatenate([(routed * TILE + slot)[None, :], rest_key], axis=0)

    vmem = pl.BlockSpec(memory_space=pltpu.VMEM)
    hbm = pl.BlockSpec(memory_space=pl.ANY)
    bf16 = jnp.bfloat16
    parcels = pltpu.VMEM((n, TILE, width), bf16)
    head, ends = pl.pallas_call(
        functools.partial(exchange_ffn, pairs, eps, cap),
        out_shape=[
            jax.ShapeDtypeStruct((tok_rows, width), bf16),
            jax.ShapeDtypeStruct((tok_rows, tail), bf16),
        ],
        in_specs=[vmem, vmem, hbm, hbm, hbm, hbm],
        out_specs=[vmem, vmem],
        scratch_shapes=[
            pltpu.VMEM((tok_rows, depth), bf16),
            parcels,
            parcels,
            parcels,
            parcels,
            pltpu.VMEM((depth, ff), bf16),
            pltpu.VMEM((depth, ff), bf16),
            pltpu.VMEM((ff, depth), bf16),
            pltpu.VMEM((GROUP * TILE, ff), bf16),
            pltpu.VMEM((GROUP * TILE, tail), bf16),
            pltpu.SemaphoreType.DMA((1,)),
            pltpu.SemaphoreType.DMA((3,)),
            pltpu.SemaphoreType.DMA((2,)),
            pltpu.SemaphoreType.DMA((n,)),
            pltpu.SemaphoreType.DMA((n,)),
            pltpu.SemaphoreType.DMA((n,)),
            pltpu.SemaphoreType.DMA((n,)),
        ],
        compiler_params=pltpu.CompilerParams(
            collective_id=0, has_side_effects=True, vmem_limit_bytes=56 * 1024 * 1024
        ),
        name="exchange_ffn",
    )(keys, keys.T, tokens, w_gate, w_up, w_down)
    return jnp.concatenate([head, ends], axis=1)


def plain(tokens, routed, slot, w_gate, w_up, w_down, experts, capacity):
    position = routed * capacity + slot
    outgoing = (
        jnp.zeros((experts * capacity, tokens.shape[1]), jnp.bfloat16).at[position].set(tokens)
    )
    parcel = lax.all_to_all(
        outgoing.reshape(experts, capacity, outgoing.shape[1]),
        ("pair", "ep"), split_axis=0, concat_axis=0, tiled=True,
    )
    flat_rows = parcel.reshape(experts * capacity, parcel.shape[2])
    gate_proj = dot(flat_rows, w_gate[0])
    up_proj = dot(flat_rows, w_up[0])
    hidden = (jax.nn.silu(gate_proj) * up_proj).astype(jnp.bfloat16)
    result = dot(hidden, w_down[0]).astype(jnp.bfloat16)
    returned = lax.all_to_all(
        result.reshape(experts, capacity, result.shape[1]),
        ("pair", "ep"), split_axis=0, concat_axis=0, tiled=True,
    )
    return jnp.take(returned.reshape(experts * capacity, -1), position, axis=0)


def shards(tokens, expert_of, w_gate, w_up, w_down):
    pairs = lax.axis_size("pair")
    eps = lax.axis_size("ep")
    experts = pairs * eps
    tok_rows, depth = tokens.shape
    cap = tok_rows // experts + tok_rows // (2 * experts)
    routed = expert_of[:, 0]
    onehot = (routed[:, None] == jnp.arange(experts, dtype=jnp.int32)[None, :]).astype(jnp.float32)
    order = jnp.arange(tok_rows)
    earlier = (order[:, None] > order[None, :]).astype(jnp.bfloat16)
    before = dot(earlier, onehot.astype(jnp.bfloat16))
    slot = jnp.sum(before * onehot, axis=1).astype(jnp.int32)
    spare = TILE - cap
    packs = 0 < spare <= cap and cap % spare == 0 and (depth * spare) % (TILE * 256) == 0
    if packs and experts % GROUP == 0 and w_gate.shape[2] % 256 == 0:
        return fused(tokens, routed, slot, w_gate, w_up, w_down, pairs, eps, cap)
    return plain(tokens, routed, slot, w_gate, w_up, w_down, experts, cap)


def solution(mesh):
    spec2 = P(("pair", "ep"), None)
    spec3 = P(("pair", "ep"), None, None)
    return jax.shard_map(
        shards,
        mesh=mesh,
        in_specs=(spec2, spec2, spec3, spec3, spec3),
        out_specs=spec2,
        check_vma=False,
    )
```

profile of v0, /device:TPU:12, one launch (start us, length us, event | category | flops | bytes accessed | tf_op | source)
XLA Modules:
  0.0 159.3 jit_solution(7596673411855083095)
XLA Ops:
  0.0 1.0 fusion
  1.0 0.7 bitcast_add_fusion
  1.7 0.7 and_select_fusion.1
  2.4 0.0 copy-start
  2.4 0.8 copy.10
  3.2 0.0 copy-done
  3.2 153.1 %exchange_ffn.1 = (bf16[256,3072]{1,0:T(8,128)(2,1)}, bf16[256,1024]{1,0:T(8,128)(2,1)}) custom-call(s32[4,256]{1,0:T(4,128)} %copy-done, s32[256,4]{1,0:T(8,128)} %bitcast.5, bf16[256,4096]{1,0:T(8,128)(2,1)} %tok_hbm.1, bf16[1,4096,768]{2,1,0:T(8,128)(2,1)} %gate_hbm.1, bf16[1,4096,768]{2,1,0:T(8,128)(2,1)} %up_hbm.1, bf16[1,768,4096]{2,1,0:T(8,128)(2,1)} %down_hbm.1), custom_call_target="tpu_custom_call" | custom-call | tf_op jit(solution)/shard_map/exchange_ffn/pallas_call | solution.py:240
  156.3 3.1 %pad_maximum_fusion = bf16[256,4096]{1,0:T(8,128)(2,1)} fusion(bf16[256,1024]{1,0:T(8,128)(2,1)} %get-tuple-element.8, bf16[256,3072]{1,0:T(8,128)(2,1)} %get-tuple-element.7), kind=kLoop, calls=%fused_computation | loop fusion | flops 4194304 | bytes 4194304 | tf_op jit(solution)/shard_map/concatenate | solution.py:272
  (3 shorter events, 0.0 us)
Async XLA Ops:
  2.4 0.8 copy-start
where the time goes:
time: 160 us; the launch traced here: 159 us
  Pallas kernels  153 us (96%)
  other arithmetic  4.48 us (3%)
    pallas_call x1, Pallas kernels, fused(): pl.pallas_call(functools.partial(exchange_ffn, pairs, eps, cap), out_shap...  153 us

commit v1 on v0

--- a/solution.py
+++ b/solution.py
@@ -293,13 +293,352 @@
     return jnp.take(returned.reshape(experts * capacity, -1), position, axis=0)
 
 
-def shards(tokens, expert_of, w_gate, w_up, w_down):
-    pairs = lax.axis_size("pair")
-    eps = lax.axis_size("ep")
+BLOCK = 8
+
+
+def near_ffn(
+    pairs, eps, spill, keys_ref, tok_hbm, gate_hbm, up_hbm, down_hbm, out_hbm, flag_ref,
+    tok, send_b, recv_b, res_b, ret_b, send_x, recv_x, res_x, ret_x, send_s, recv_s, res_s, ret_s,
+    note, notes, gate, up, down, rows_x, hidden, total,
+    tok_sem, w_sem, out_sem, ssem_b, rsem_b, ssem_x, rsem_x, ssem_s, rsem_s, ssem_n, rsem_n,
+):
+    n = pairs * eps
+    near = n // 2
+    line = eps // 2
+    pair, ep = lax.axis_index("pair"), lax.axis_index("ep")
+    side, spot = ep // line, ep % line
+    tok_rows, depth = tok.shape
+    mid = depth // 2
+    ff = hidden.shape[1]
+    extra = BLOCK // 2
+    bf16, f32, i32 = jnp.bfloat16, jnp.float32, jnp.int32
+    none = -4 * n * TILE
+    wide = 512
+
+    def peer(k, sign):
+        j = k % near + 1
+        p = lax.rem(pair + pairs + sign * (j // line % pairs), pairs)
+        s = lax.rem(spot + line + sign * (j % line), line)
+        return p, lax.rem(side + 1 - k // near, 2) * line + s
+
+    tok_load = pltpu.make_async_copy(tok_hbm, tok, tok_sem.at[0])
+    tok_load.start()
+    barrier = pltpu.get_barrier_semaphore()
+
+    @pl.loop(0, n - 1)
+    def _(k):
+        pl.semaphore_signal(barrier, inc=1, device_id=peer(k, 1), device_id_type=MESH)
+
+    loads = [
+        pltpu.make_async_copy(src.at[0], dst, w_sem.at[i])
+        for i, (src, dst) in enumerate(((gate_hbm, gate), (up_hbm, up), (down_hbm, down)))
+    ]
+    for load in loads:
+        load.start()
+
+    def remote(src, dst, ssem, rsem, to):
+        return pltpu.make_async_remote_copy(
+            src_ref=src, dst_ref=dst, send_sem=ssem, recv_sem=rsem,
+            device_id=to, device_id_type=MESH,
+        )
+
+    def out_b(k):
+        return remote(send_b.at[k], recv_b.at[k], ssem_b.at[0, k], rsem_b.at[0, k], peer(k, 1))
+
+    def back_b(k):
+        return remote(res_b.at[k], ret_b.at[k], ssem_b.at[1, k], rsem_b.at[1, k], peer(k, -1))
+
+    def out_x(k):
+        return remote(
+            send_x.at[k], recv_x.at[k], ssem_x.at[0, k], rsem_x.at[0, k], peer(k + near, 1)
+        )
+
+    def back_x(k):
+        return remote(
+            res_x.at[k], ret_x.at[k], ssem_x.at[1, k], rsem_x.at[1, k], peer(k + near, -1)
+        )
+
+    mirror = (pair, lax.rem(side + 1, 2) * line + spot)
+    out_s = remote(send_s, recv_s, ssem_s.at[0], rsem_s.at[0], mirror)
+    back_s = remote(res_s, ret_s, ssem_s.at[1], rsem_s.at[1], mirror)
+
+    def tell(k):
+        return remote(note, notes.at[k], ssem_n.at[k], rsem_n.at[k], peer(k, 1))
+
+    def iota(shape, axis):
+        return lax.broadcasted_iota(i32, shape, axis)
+
+    def one_hot(mask):
+        return jnp.where(mask, 1.0, 0.0).astype(bf16)
+
+    expert = iota((n, 128), 0)
+    order = jnp.zeros((n, 128), i32)
+    for k in range(n):
+        p, e = peer(k, 1) if k < n - 1 else (pair, ep)
+        order = jnp.where(expert == p * eps + e, k, order)
+    order = order.astype(f32)
+    routed = keys_ref[0:1, :]
+    chosen = jnp.where(iota((n, tok_rows), 0) == routed, 1.0, 0.0)
+    earlier = one_hot(iota((tok_rows, tok_rows), 0) < iota((tok_rows, tok_rows), 1))
+    before = dot(chosen.astype(bf16), earlier)
+    load_of = jnp.sum(chosen, axis=1, keepdims=True)
+    over = jnp.where(order < near, jnp.maximum(load_of - BLOCK, 0.0), 0.0)
+    lower = one_hot(iota((n, n), 1) < iota((n, n), 0))
+    start = dot(lower, over.astype(bf16))
+    slot = jnp.sum(chosen * before, axis=0, keepdims=True).astype(i32)
+    rank = jnp.sum(chosen * order[:, 0:1], axis=0, keepdims=True).astype(i32)
+    first = jnp.sum(chosen * start[:, 0:1], axis=0, keepdims=True).astype(i32)
+    far = rank < near
+    direct = slot < BLOCK
+    spot_s = first + slot - BLOCK
+    spilled = far & (slot >= BLOCK)
+    base_key = jnp.where(far & direct, rank * BLOCK + slot, none)
+    far_key = jnp.where(spilled, near * BLOCK + spot_s, base_key)
+    close_key = jnp.where(direct, (rank - near) * BLOCK + slot, (rank - near) * BLOCK + near * BLOCK + slot - BLOCK)
+    close_key = jnp.where(far, none, close_key)
+    pack_b = jnp.where(direct, rank * TILE + slot, none)
+    pack_x = jnp.where(direct | far, none, (rank - near) * TILE + slot - BLOCK)
+    pack_s = jnp.where(spilled, spot_s // BLOCK * TILE + spot_s % BLOCK, none)
+    home = rank * TILE + extra + slot - BLOCK + 1
+    lines = jnp.concatenate([pack_b, pack_x, pack_s, home, pack_b, pack_b, pack_b, pack_b], axis=0)
+    cols = jnp.transpose(lines.astype(f32)).astype(i32)
+    col_b, col_x, col_s, col_h = (cols[:, i:i + 1] for i in range(4))
+    lane = iota((tok_rows, 128), 1)
+    codes = jnp.where(col_s == lane, col_h, 0) + jnp.where(col_s + BLOCK == lane, col_h + BLOCK, 0)
+    codes = jnp.sum(codes.astype(f32), axis=0, keepdims=True)
+    excess = jnp.sum(over[:, 0:1], axis=0, keepdims=True) > spill * BLOCK
+    excess = jnp.where(excess, 1.0, 0.0)
+    note[...] = jnp.where(iota((1, 128), 1) == 127, excess, codes)
+
+    def split(at, chunk):
+        return pl.ds(pl.multiple_of(at + chunk * wide, wide), wide)
+
+    def weave(left, right, count):
+        left = left.reshape(count, BLOCK, wide)
+        right = right.reshape(count, BLOCK, wide)
+        return jnp.concatenate([left, right], axis=1).astype(bf16)
+
+    tok_load.wait()
+    far_hot = one_hot(far_key == iota((near * BLOCK + 2 * TILE, tok_rows), 0))
+
+    @pl.loop(0, mid // wide)
+    def _(c):
+        left = dot(far_hot, tok[:, split(0, c)])
+        right = dot(far_hot, tok[:, split(mid, c)])
+        body = near * BLOCK
+        send_b[pl.ds(0, near), :, split(0, c)] = weave(left[:body], right[:body], near)
+        body, stop = near * BLOCK, near * BLOCK + spill * BLOCK
+        send_s[:, :, split(0, c)] = weave(left[body:stop], right[body:stop], spill)
+
+    pl.semaphore_wait(barrier, n - 1)
+    tell(near - 1).start()
+    out_s.start()
+
+    @pl.loop(0, near)
+    def _(k):
+        out_b(k).start()
+
+    close_hot = one_hot(close_key == iota((2 * near * BLOCK, tok_rows), 0))
+
+    @pl.loop(0, mid // wide)
+    def _(c):
+        left = dot(close_hot, tok[:, split(0, c)])
+        right = dot(close_hot, tok[:, split(mid, c)])
+        body = near * BLOCK
+        send_b[pl.ds(near, near), :, split(0, c)] = weave(left[:body], right[:body], near)
+        send_x[:, :, split(0, c)] = weave(left[body:], right[body:], near)
+
+    @pl.loop(near, n - 1)
+    def _(k):
+        out_b(k).start()
+
+    recv_b[n - 1] = send_b[n - 1]
+
+    tell(near - 1).wait_recv()
+    out_s.wait_recv()
+    code = notes[near - 1]
+    depth_s = spill * TILE
+    placed = code[:, :depth_s].astype(i32) - 1
+    place_hot = one_hot(placed == iota((near * TILE, depth_s), 0))
+
+    @pl.loop(0, mid // wide)
+    def _(c):
+        moved = dot(place_hot, recv_s[:, :, split(0, c)].reshape(depth_s, wide))
+        mine = send_x[:, :, split(0, c)].reshape(near * TILE, wide).astype(f32)
+        send_x[:, :, split(0, c)] = (mine + moved).astype(bf16).reshape(near, TILE, wide)
+
+    @pl.loop(0, near - 1)
+    def _(k):
+        out_x(k).start()
+
+    recv_x[near - 1] = send_x[near - 1]
+
+    @pl.loop(0, near - 1)
+    def _(k):
+        tell(k).start()
+
+    @pl.loop(near, n - 1)
+    def _(k):
+        tell(k).start()
+
+    diagonal = iota((depth_s, 128), 0) == iota((depth_s, 128), 1)
+    wanted = jnp.sum(jnp.where(diagonal, code, 0.0), axis=1, keepdims=True).astype(i32) - 1
+    fetch_hot = one_hot(wanted == iota((depth_s, near * TILE), 1))
+
+    for load in loads:
+        load.wait()
+
+    def ffn(arrived, result, base, count):
+        rows = count * BLOCK
+
+        @pl.loop(0, mid // wide)
+        def _(c):
+            piece = arrived[pl.ds(base, count), :, split(0, c)].astype(f32)
+            rows_x[:rows, split(0, c)] = piece[:, :BLOCK].reshape(rows, wide).astype(bf16)
+            rows_x[:rows, split(mid, c)] = piece[:, BLOCK:].reshape(rows, wide).astype(bf16)
+
+        step = 256
+
+        @pl.loop(0, ff // step)
+        def _(f):
+            at = pl.ds(pl.multiple_of(f * step, step), step)
+            g_out = dot(rows_x[:rows, :], gate[:, at])
+            u_out = dot(rows_x[:rows, :], up[:, at])
+            hidden[:rows, at] = (jax.nn.silu(g_out) * u_out).astype(bf16)
+
+        @pl.loop(0, mid // wide)
+        def _(c):
+            left = dot(hidden[:rows, :], down[:, split(0, c)])
+            right = dot(hidden[:rows, :], down[:, split(mid, c)])
+            result[pl.ds(base, count), :, split(0, c)] = weave(left, right, count)
+
+    def each(first, last, act):
+        @pl.loop(first, last)
+        def _(k):
+            act(k)
+
+    def unpack(col, returned, base, count, start, ship):
+        depth_k = count * TILE
+        at = iota((tok_rows, depth_k), 1) + base * TILE
+        left_hot = one_hot(col == at)
+        right_hot = one_hot(col + BLOCK == at)
+
+        @pl.loop(0, mid // wide)
+        def _(c):
+            piece = returned[pl.ds(base, count), :, split(0, c)].reshape(depth_k, wide)
+            for hot, half in ((left_hot, 0), (right_hot, mid)):
+                got = dot(hot, piece).astype(bf16)
+                total[:, split(half, c)] = got if start else total[:, split(half, c)] + got
+                if ship:
+                    written(half, c).start()
+
+    def written(half, c):
+        at = split(half, c)
+        sem = out_sem.at[half // mid, c]
+        return pltpu.make_async_copy(total.at[:, at], out_hbm.at[:, at], sem)
+
+    each(near, n - 1, lambda k: out_b(k).wait_recv())
+    ffn(recv_b, res_b, near, near)
+    each(near, n - 1, lambda k: back_b(k).start())
+    ret_b[n - 1] = res_b[n - 1]
+    each(0, near // 2, lambda k: out_b(k).wait_recv())
+    ffn(recv_b, res_b, 0, near // 2)
+    each(0, near // 2, lambda k: back_b(k).start())
+    each(0, near - 1, lambda k: out_x(k).wait_recv())
+    ffn(recv_x, res_x, 0, near)
+    each(0, near - 1, lambda k: back_x(k).start())
+    ret_x[near - 1] = res_x[near - 1]
+    each(near // 2, near, lambda k: out_b(k).wait_recv())
+    ffn(recv_b, res_b, near // 2, near // 2)
+    each(near // 2, near, lambda k: back_b(k).start())
+
+    each(0, near - 1, lambda k: back_x(k).wait_recv())
+
+    @pl.loop(0, mid // wide)
+    def _(c):
+        piece = ret_x[:, :, split(0, c)].reshape(near * TILE, wide)
+        res_s[:, :, split(0, c)] = dot(fetch_hot, piece).astype(bf16).reshape(spill, TILE, wide)
+
+    back_s.start()
+    unpack(col_x, ret_x, 0, near, True, False)
+    each(near, n - 1, lambda k: back_b(k).wait_recv())
+    unpack(col_b, ret_b, near, near, False, False)
+    each(0, near - 1, lambda k: tell(k).wait_recv())
+    each(near, n - 1, lambda k: tell(k).wait_recv())
+    notes[n - 1] = note[...]
+    worst = jnp.max(notes[...], axis=0)
+    flag_ref[...] = jnp.broadcast_to(worst, flag_ref.shape)
+    each(0, near // 2, lambda k: back_b(k).wait_recv())
+    unpack(col_b, ret_b, 0, near // 2, False, False)
+    each(near // 2, near, lambda k: back_b(k).wait_recv())
+    unpack(col_b, ret_b, near // 2, near // 2, False, False)
+    back_s.wait_recv()
+    unpack(col_s, ret_s, 0, spill, False, True)
+
+    each(0, n - 1, lambda k: out_b(k).wait_send())
+    each(0, n - 1, lambda k: back_b(k).wait_send())
+    each(0, n - 1, lambda k: tell(k).wait_send())
+    each(0, near - 1, lambda k: out_x(k).wait_send())
+    each(0, near - 1, lambda k: back_x(k).wait_send())
+    out_s.wait_send()
+    back_s.wait_send()
+
+    @pl.loop(0, mid // wide)
+    def _(c):
+        written(0, c).wait()
+        written(mid, c).wait()
+
+
+def spilling(tokens, routed, w_gate, w_up, w_down, pairs, eps):
+    n = pairs * eps
+    near = n // 2
+    tok_rows, depth = tokens.shape
+    ff = w_gate.shape[2]
+    spill = 3
+    bf16, f32 = jnp.bfloat16, jnp.float32
+    vmem = pl.BlockSpec(memory_space=pltpu.VMEM)
+    hbm = pl.BlockSpec(memory_space=pl.ANY)
+    dma = pltpu.SemaphoreType.DMA
+
+    def blocks(count):
+        return pltpu.VMEM((count, TILE, depth // 2), bf16)
+
+    return pl.pallas_call(
+        functools.partial(near_ffn, pairs, eps, spill),
+        out_shape=[
+            jax.ShapeDtypeStruct((tok_rows, depth), bf16),
+            jax.ShapeDtypeStruct((8, 128), f32),
+        ],
+        in_specs=[vmem, hbm, hbm, hbm, hbm],
+        out_specs=[hbm, vmem],
+        scratch_shapes=[
+            pltpu.VMEM((tok_rows, depth), bf16),
+            *[blocks(n)] * 4,
+            *[blocks(near)] * 4,
+            *[blocks(spill)] * 4,
+            pltpu.VMEM((1, 128), f32),
+            pltpu.VMEM((n, 1, 128), f32),
+            pltpu.VMEM((depth, ff), bf16),
+            pltpu.VMEM((depth, ff), bf16),
+            pltpu.VMEM((ff, depth), bf16),
+            pltpu.VMEM((near * BLOCK, depth), bf16),
+            pltpu.VMEM((near * BLOCK, ff), bf16),
+            pltpu.VMEM((tok_rows, depth), bf16),
+            dma((1,)), dma((3,)), dma((2, depth // 2 // 512)),
+            dma((2, n)), dma((2, n)), dma((2, near)), dma((2, near)),
+            dma((2,)), dma((2,)), dma((n,)), dma((n,)),
+        ],
+        compiler_params=pltpu.CompilerParams(
+            collective_id=1, has_side_effects=True, vmem_limit_bytes=56 * 1024 * 1024
+        ),
+        name="near_ffn",
+    )(routed.reshape(1, tok_rows), tokens, w_gate, w_up, w_down)
+
+
+def dispatch(tokens, routed, w_gate, w_up, w_down, pairs, eps):
     experts = pairs * eps
     tok_rows, depth = tokens.shape
     cap = tok_rows // experts + tok_rows // (2 * experts)
-    routed = expert_of[:, 0]
     onehot = (routed[:, None] == jnp.arange(experts, dtype=jnp.int32)[None, :]).astype(jnp.float32)
     order = jnp.arange(tok_rows)
     earlier = (order[:, None] > order[None, :]).astype(jnp.bfloat16)
@@ -312,6 +651,24 @@
     return plain(tokens, routed, slot, w_gate, w_up, w_down, experts, cap)
 
 
+def shards(tokens, expert_of, w_gate, w_up, w_down):
+    pairs = lax.axis_size("pair")
+    eps = lax.axis_size("ep")
+    experts = pairs * eps
+    tok_rows, depth = tokens.shape
+    routed = expert_of[:, 0]
+    whole = (tokens, routed, w_gate, w_up, w_down)
+    even = tok_rows == BLOCK * experts and eps % 2 == 0 and experts % (2 * GROUP) == 0
+    if not (even and depth % 1024 == 0 and w_gate.shape[2] % 256 == 0):
+        return dispatch(*whole, pairs, eps)
+    result, flag = spilling(*whole, pairs, eps)
+    return lax.cond(
+        flag[0, 127] > 0,
+        lambda: dispatch(*whole, pairs, eps),
+        lambda: result,
+    )
+
+
 def solution(mesh):
     spec2 = P(("pair", "ep"), None)
     spec3 = P(("pair", "ep"), None, None)

time: 160 us -> 130 us (0.81)
  the two profiles are of different devices: /device:TPU:12 before, /device:TPU:0 now
where the time goes in v1:
time: 130 us
  Pallas kernels  127 us (98%)
  local copies, waits for them, and re-layouts  2.59 us (2%)
    pallas_call x1, Pallas kernels, spilling(): pl.pallas_call(functools.partial(near_ffn, pairs, eps, spill), out_shape=...  127 us

profile of v1, /device:TPU:0, one launch (start us, length us, event | category | flops | bytes accessed | tf_op | source)
XLA Modules:
  0.0 130.2 jit_solution(7882637373055153371)
XLA Ops:
  0.0 0.0 copy-start
  0.0 0.0 copy-start.2
  0.0 126.7 %near_ffn.1 = (bf16[256,4096]{1,0:T(8,128)(2,1)S(1)}, f32[8,128]{1,0:T(8,128)}) custom-call(s32[1,256]{1,0:T(1,128)} %bitcast.9, bf16[256,4096]{1,0:T(8,128)(2,1)} %tok_hbm.1, bf16[1,4096,768]{2,1,0:T(8,128)(2,1)} %gate_hbm.1, bf16[1,4096,768]{2,1,0:T(8,128)(2,1)} %up_hbm.1, bf16[1,768,4096]{2,1,0:T(8,128)(2,1)} %down_hbm.1), custom_call_target="tpu_custom_call" | custom-call | tf_op jit(solution)/shard_map/near_ffn/pallas_call | solution.py:606
  126.7 1.3 slice.3
  128.6 0.0 copy-done
  128.6 0.0 copy-done.2
  128.6 0.2 conditional.1
  128.8 1.3 %copy.15 = bf16[256,4096]{1,0:T(8,128)(2,1)} copy(bf16[256,4096]{1,0:T(8,128)(2,1)S(1)} %get-tuple-element.33) | data formatting | bytes 4194304
Async XLA Ops:
  0.0 128.6 %copy-start = (bf16[256,4096]{1,0:T(8,128)(2,1)S(1)}, bf16[256,4096]{1,0:T(8,128)(2,1)}, u32[]{:S(2)}) copy-start(bf16[256,4096]{1,0:T(8,128)(2,1)} %tok_hbm.1) | copy-start | bytes 6291460
  0.0 128.6 %copy-start.2 = (s32[256,1]{0,1:T(1,128)S(1)}, s32[256,1]{0,1:T(1,128)}, u32[]{:S(2)}) copy-start(s32[256,1]{0,1:T(1,128)} %param.8) | copy-start | bytes 3076

commit v2 on v1

--- a/solution.py
+++ b/solution.py
@@ -297,10 +297,10 @@
 
 
 def near_ffn(
-    pairs, eps, spill, keys_ref, tok_hbm, gate_hbm, up_hbm, down_hbm, out_hbm, flag_ref,
+    pairs, eps, spill, keys_hbm, tok_hbm, gate_hbm, up_hbm, down_hbm, total, flag_ref,
     tok, send_b, recv_b, res_b, ret_b, send_x, recv_x, res_x, ret_x, send_s, recv_s, res_s, ret_s,
-    note, notes, gate, up, down, rows_x, hidden, total,
-    tok_sem, w_sem, out_sem, ssem_b, rsem_b, ssem_x, rsem_x, ssem_s, rsem_s, ssem_n, rsem_n,
+    keys_ref, note, notes, gate, up, down, rows_x, hidden,
+    load_sem, w_sem, ssem, rsem,
 ):
     n = pairs * eps
     near = n // 2
@@ -321,7 +321,9 @@
         s = lax.rem(spot + line + sign * (j % line), line)
         return p, lax.rem(side + 1 - k // near, 2) * line + s
 
-    tok_load = pltpu.make_async_copy(tok_hbm, tok, tok_sem.at[0])
+    key_load = pltpu.make_async_copy(keys_hbm, keys_ref, load_sem.at[0])
+    key_load.start()
+    tok_load = pltpu.make_async_copy(tok_hbm, tok, load_sem.at[1])
     tok_load.start()
     barrier = pltpu.get_barrier_semaphore()
 
@@ -333,37 +335,62 @@
         pltpu.make_async_copy(src.at[0], dst, w_sem.at[i])
         for i, (src, dst) in enumerate(((gate_hbm, gate), (up_hbm, up), (down_hbm, down)))
     ]
-    for load in loads:
-        load.start()
-
-    def remote(src, dst, ssem, rsem, to):
+
+    half = near // 2
+    groups = {
+        "far_a": (send_b, recv_b, 0, half),
+        "far_b": (send_b, recv_b, half, near),
+        "close": (send_b, recv_b, near, n - 1),
+        "extra": (send_x, recv_x, 0, near - 1),
+        "spill": (send_s, recv_s, 0, spill),
+        "back_far_a": (res_b, ret_b, 0, half),
+        "back_far_b": (res_b, ret_b, half, near),
+        "back_close": (res_b, ret_b, near, n - 1),
+        "back_extra": (res_x, ret_x, 0, near - 1),
+        "back_spill": (res_s, ret_s, 0, spill),
+    }
+    ports = {name: i for i, name in enumerate(groups)}
+
+    def remote(name, src, dst, to, part=0):
+        at = ports[name] + part
         return pltpu.make_async_remote_copy(
-            src_ref=src, dst_ref=dst, send_sem=ssem, recv_sem=rsem,
+            src_ref=src, dst_ref=dst, send_sem=ssem.at[at], recv_sem=rsem.at[at],
             device_id=to, device_id_type=MESH,
         )
 
-    def out_b(k):
-        return remote(send_b.at[k], recv_b.at[k], ssem_b.at[0, k], rsem_b.at[0, k], peer(k, 1))
-
-    def back_b(k):
-        return remote(res_b.at[k], ret_b.at[k], ssem_b.at[1, k], rsem_b.at[1, k], peer(k, -1))
-
-    def out_x(k):
-        return remote(
-            send_x.at[k], recv_x.at[k], ssem_x.at[0, k], rsem_x.at[0, k], peer(k + near, 1)
+    mirror = (pair, lax.rem(side + 1, 2) * line + spot)
+
+    def go(name):
+        src, dst, low, high = groups[name]
+        if src.shape[0] == spill:
+            remote(name, src, dst, mirror).start()
+            return
+        sign = -1 if name[:4] == "back" else 1
+        skip = near if src.shape[0] == near else 0
+
+        @pl.loop(low, high)
+        def _(k):
+            remote(name, src.at[k], dst.at[k], peer(k + skip, sign)).start()
+
+    def group(name):
+        src, dst, low, high = groups[name]
+        part = pl.ds(low, high - low)
+        return remote(name, src.at[part], dst.at[part], mirror)
+
+    last = len(groups)
+
+    def tell(k, part):
+        return pltpu.make_async_remote_copy(
+            src_ref=note, dst_ref=notes.at[k], send_sem=ssem.at[last + part],
+            recv_sem=rsem.at[last + part], device_id=peer(k, 1), device_id_type=MESH,
         )
 
-    def back_x(k):
-        return remote(
-            res_x.at[k], ret_x.at[k], ssem_x.at[1, k], rsem_x.at[1, k], peer(k + near, -1)
+    def told(low, high, part):
+        some = notes.at[pl.ds(low, high - low)]
+        return pltpu.make_async_remote_copy(
+            src_ref=some, dst_ref=some, send_sem=ssem.at[last + part],
+            recv_sem=rsem.at[last + part], device_id=mirror, device_id_type=MESH,
         )
-
-    mirror = (pair, lax.rem(side + 1, 2) * line + spot)
-    out_s = remote(send_s, recv_s, ssem_s.at[0], rsem_s.at[0], mirror)
-    back_s = remote(res_s, ret_s, ssem_s.at[1], rsem_s.at[1], mirror)
-
-    def tell(k):
-        return remote(note, notes.at[k], ssem_n.at[k], rsem_n.at[k], peer(k, 1))
 
     def iota(shape, axis):
         return lax.broadcasted_iota(i32, shape, axis)
@@ -377,25 +404,50 @@
         p, e = peer(k, 1) if k < n - 1 else (pair, ep)
         order = jnp.where(expert == p * eps + e, k, order)
     order = order.astype(f32)
-    routed = keys_ref[0:1, :]
-    chosen = jnp.where(iota((n, tok_rows), 0) == routed, 1.0, 0.0)
+    key_load.wait()
+    routed = keys_ref[...]
+    which = iota((n, tok_rows), 0)
+    chosen = jnp.where(which == routed, 1.0, 0.0)
     earlier = one_hot(iota((tok_rows, tok_rows), 0) < iota((tok_rows, tok_rows), 1))
     before = dot(chosen.astype(bf16), earlier)
     load_of = jnp.sum(chosen, axis=1, keepdims=True)
     over = jnp.where(order < near, jnp.maximum(load_of - BLOCK, 0.0), 0.0)
-    lower = one_hot(iota((n, n), 1) < iota((n, n), 0))
-    start = dot(lower, over.astype(bf16))
+    ahead = jnp.where(which < routed, over[:, 0:1], 0.0)
+    first = jnp.sum(ahead, axis=0, keepdims=True).astype(i32)
+    rank = jnp.sum(chosen * order[:, 0:1], axis=0, keepdims=True).astype(i32)
     slot = jnp.sum(chosen * before, axis=0, keepdims=True).astype(i32)
-    rank = jnp.sum(chosen * order[:, 0:1], axis=0, keepdims=True).astype(i32)
-    first = jnp.sum(chosen * start[:, 0:1], axis=0, keepdims=True).astype(i32)
     far = rank < near
     direct = slot < BLOCK
     spot_s = first + slot - BLOCK
     spilled = far & (slot >= BLOCK)
-    base_key = jnp.where(far & direct, rank * BLOCK + slot, none)
-    far_key = jnp.where(spilled, near * BLOCK + spot_s, base_key)
-    close_key = jnp.where(direct, (rank - near) * BLOCK + slot, (rank - near) * BLOCK + near * BLOCK + slot - BLOCK)
-    close_key = jnp.where(far, none, close_key)
+    spill_key = jnp.where(spilled, spot_s, none)
+
+    def split(at, chunk):
+        return pl.ds(pl.multiple_of(at + chunk * wide, wide), wide)
+
+    def weave(left, right, count):
+        left = left.reshape(count, BLOCK, wide)
+        right = right.reshape(count, BLOCK, wide)
+        return jnp.concatenate([left, right], axis=1).astype(bf16)
+
+    tok_load.wait()
+    for load in loads:
+        load.start()
+
+    spill_hot = one_hot(spill_key == iota((spill * BLOCK, tok_rows), 0))
+
+    @pl.loop(0, mid // wide)
+    def _(c):
+        left = dot(spill_hot, tok[:, split(0, c)])
+        right = dot(spill_hot, tok[:, split(mid, c)])
+        send_s[:, :, split(0, c)] = weave(left, right, spill)
+
+    pl.semaphore_wait(barrier, n - 1)
+    go("spill")
+
+    far_key = jnp.where(far & direct, rank * BLOCK + slot, none)
+    beyond = jnp.where(direct, slot, near * BLOCK + slot - BLOCK)
+    close_key = jnp.where(far, none, (rank - near) * BLOCK + beyond)
     pack_b = jnp.where(direct, rank * TILE + slot, none)
     pack_x = jnp.where(direct | far, none, (rank - near) * TILE + slot - BLOCK)
     pack_s = jnp.where(spilled, spot_s // BLOCK * TILE + spot_s % BLOCK, none)
@@ -410,33 +462,17 @@
     excess = jnp.where(excess, 1.0, 0.0)
     note[...] = jnp.where(iota((1, 128), 1) == 127, excess, codes)
 
-    def split(at, chunk):
-        return pl.ds(pl.multiple_of(at + chunk * wide, wide), wide)
-
-    def weave(left, right, count):
-        left = left.reshape(count, BLOCK, wide)
-        right = right.reshape(count, BLOCK, wide)
-        return jnp.concatenate([left, right], axis=1).astype(bf16)
-
-    tok_load.wait()
-    far_hot = one_hot(far_key == iota((near * BLOCK + 2 * TILE, tok_rows), 0))
+    tell(near - 1, 0).start()
+    far_hot = one_hot(far_key == iota((near * BLOCK, tok_rows), 0))
 
     @pl.loop(0, mid // wide)
     def _(c):
         left = dot(far_hot, tok[:, split(0, c)])
         right = dot(far_hot, tok[:, split(mid, c)])
-        body = near * BLOCK
-        send_b[pl.ds(0, near), :, split(0, c)] = weave(left[:body], right[:body], near)
-        body, stop = near * BLOCK, near * BLOCK + spill * BLOCK
-        send_s[:, :, split(0, c)] = weave(left[body:stop], right[body:stop], spill)
-
-    pl.semaphore_wait(barrier, n - 1)
-    tell(near - 1).start()
-    out_s.start()
-
-    @pl.loop(0, near)
-    def _(k):
-        out_b(k).start()
+        send_b[pl.ds(0, near), :, split(0, c)] = weave(left, right, near)
+
+    go("far_a")
+    go("far_b")
 
     close_hot = one_hot(close_key == iota((2 * near * BLOCK, tok_rows), 0))
 
@@ -448,14 +484,12 @@
         send_b[pl.ds(near, near), :, split(0, c)] = weave(left[:body], right[:body], near)
         send_x[:, :, split(0, c)] = weave(left[body:], right[body:], near)
 
-    @pl.loop(near, n - 1)
-    def _(k):
-        out_b(k).start()
+    go("close")
 
     recv_b[n - 1] = send_b[n - 1]
 
-    tell(near - 1).wait_recv()
-    out_s.wait_recv()
+    tell(near - 1, 0).wait_recv()
+    group("spill").wait_recv()
     code = notes[near - 1]
     depth_s = spill * TILE
     placed = code[:, :depth_s].astype(i32) - 1
@@ -467,19 +501,16 @@
         mine = send_x[:, :, split(0, c)].reshape(near * TILE, wide).astype(f32)
         send_x[:, :, split(0, c)] = (mine + moved).astype(bf16).reshape(near, TILE, wide)
 
+    go("extra")
+    recv_x[near - 1] = send_x[near - 1]
+
     @pl.loop(0, near - 1)
     def _(k):
-        out_x(k).start()
-
-    recv_x[near - 1] = send_x[near - 1]
-
-    @pl.loop(0, near - 1)
-    def _(k):
-        tell(k).start()
+        tell(k, 1).start()
 
     @pl.loop(near, n - 1)
     def _(k):
-        tell(k).start()
+        tell(k, 2).start()
 
     diagonal = iota((depth_s, 128), 0) == iota((depth_s, 128), 1)
     wanted = jnp.sum(jnp.where(diagonal, code, 0.0), axis=1, keepdims=True).astype(i32) - 1
@@ -512,12 +543,7 @@
             right = dot(hidden[:rows, :], down[:, split(mid, c)])
             result[pl.ds(base, count), :, split(0, c)] = weave(left, right, count)
 
-    def each(first, last, act):
-        @pl.loop(first, last)
-        def _(k):
-            act(k)
-
-    def unpack(col, returned, base, count, start, ship):
+    def unpack(col, returned, base, count, start):
         depth_k = count * TILE
         at = iota((tok_rows, depth_k), 1) + base * TILE
         left_hot = one_hot(col == at)
@@ -529,64 +555,51 @@
             for hot, half in ((left_hot, 0), (right_hot, mid)):
                 got = dot(hot, piece).astype(bf16)
                 total[:, split(half, c)] = got if start else total[:, split(half, c)] + got
-                if ship:
-                    written(half, c).start()
-
-    def written(half, c):
-        at = split(half, c)
-        sem = out_sem.at[half // mid, c]
-        return pltpu.make_async_copy(total.at[:, at], out_hbm.at[:, at], sem)
-
-    each(near, n - 1, lambda k: out_b(k).wait_recv())
+
+    group("close").wait_recv()
     ffn(recv_b, res_b, near, near)
-    each(near, n - 1, lambda k: back_b(k).start())
+    go("back_close")
     ret_b[n - 1] = res_b[n - 1]
-    each(0, near // 2, lambda k: out_b(k).wait_recv())
-    ffn(recv_b, res_b, 0, near // 2)
-    each(0, near // 2, lambda k: back_b(k).start())
-    each(0, near - 1, lambda k: out_x(k).wait_recv())
+    group("far_a").wait_recv()
+    ffn(recv_b, res_b, 0, half)
+    go("back_far_a")
+    group("extra").wait_recv()
     ffn(recv_x, res_x, 0, near)
-    each(0, near - 1, lambda k: back_x(k).start())
+    go("back_extra")
     ret_x[near - 1] = res_x[near - 1]
-    each(near // 2, near, lambda k: out_b(k).wait_recv())
-    ffn(recv_b, res_b, near // 2, near // 2)
-    each(near // 2, near, lambda k: back_b(k).start())
-
-    each(0, near - 1, lambda k: back_x(k).wait_recv())
+    group("far_b").wait_recv()
+    ffn(recv_b, res_b, half, half)
+    go("back_far_b")
+
+    for name in ("spill", "far_a", "far_b", "close", "extra"):
+        group(name).wait_send()
+    tell(near - 1, 0).wait_send()
+    told(0, near - 1, 1).wait_send()
+    told(near, n - 1, 2).wait_send()
+    group("back_extra").wait_recv()
 
     @pl.loop(0, mid // wide)
     def _(c):
         piece = ret_x[:, :, split(0, c)].reshape(near * TILE, wide)
         res_s[:, :, split(0, c)] = dot(fetch_hot, piece).astype(bf16).reshape(spill, TILE, wide)
 
-    back_s.start()
-    unpack(col_x, ret_x, 0, near, True, False)
-    each(near, n - 1, lambda k: back_b(k).wait_recv())
-    unpack(col_b, ret_b, near, near, False, False)
-    each(0, near - 1, lambda k: tell(k).wait_recv())
-    each(near, n - 1, lambda k: tell(k).wait_recv())
+    go("back_spill")
+    unpack(col_x, ret_x, 0, near, True)
+    group("back_close").wait_recv()
+    unpack(col_b, ret_b, near, near, False)
+    told(0, near - 1, 1).wait_recv()
+    told(near, n - 1, 2).wait_recv()
     notes[n - 1] = note[...]
-    worst = jnp.max(notes[...], axis=0)
-    flag_ref[...] = jnp.broadcast_to(worst, flag_ref.shape)
-    each(0, near // 2, lambda k: back_b(k).wait_recv())
-    unpack(col_b, ret_b, 0, near // 2, False, False)
-    each(near // 2, near, lambda k: back_b(k).wait_recv())
-    unpack(col_b, ret_b, near // 2, near // 2, False, False)
-    back_s.wait_recv()
-    unpack(col_s, ret_s, 0, spill, False, True)
-
-    each(0, n - 1, lambda k: out_b(k).wait_send())
-    each(0, n - 1, lambda k: back_b(k).wait_send())
-    each(0, n - 1, lambda k: tell(k).wait_send())
-    each(0, near - 1, lambda k: out_x(k).wait_send())
-    each(0, near - 1, lambda k: back_x(k).wait_send())
-    out_s.wait_send()
-    back_s.wait_send()
-
-    @pl.loop(0, mid // wide)
-    def _(c):
-        written(0, c).wait()
-        written(mid, c).wait()
+    worst = jnp.where(iota((1, 128), 1) == 127, jnp.max(notes[...], axis=0), 0.0)
+    flag_ref[0, 0] = jnp.max(worst)
+    group("back_far_a").wait_recv()
+    unpack(col_b, ret_b, 0, half, False)
+    group("back_far_b").wait_recv()
+    unpack(col_b, ret_b, half, half, False)
+    group("back_spill").wait_recv()
+    unpack(col_s, ret_s, 0, spill, False)
+    for name in ("back_close", "back_far_a", "back_extra", "back_far_b", "back_spill"):
+        group(name).wait_send()
 
 
 def spilling(tokens, routed, w_gate, w_up, w_down, pairs, eps):
@@ -607,15 +620,16 @@
         functools.partial(near_ffn, pairs, eps, spill),
         out_shape=[
             jax.ShapeDtypeStruct((tok_rows, depth), bf16),
-            jax.ShapeDtypeStruct((8, 128), f32),
+            jax.ShapeDtypeStruct((1, 1), f32),
         ],
-        in_specs=[vmem, hbm, hbm, hbm, hbm],
-        out_specs=[hbm, vmem],
+        in_specs=[hbm, hbm, hbm, hbm, hbm],
+        out_specs=[vmem, pl.BlockSpec(memory_space=pltpu.SMEM)],
         scratch_shapes=[
             pltpu.VMEM((tok_rows, depth), bf16),
             *[blocks(n)] * 4,
             *[blocks(near)] * 4,
             *[blocks(spill)] * 4,
+            pltpu.VMEM((1, tok_rows), jnp.int32),
             pltpu.VMEM((1, 128), f32),
             pltpu.VMEM((n, 1, 128), f32),
             pltpu.VMEM((depth, ff), bf16),
@@ -623,10 +637,7 @@
             pltpu.VMEM((ff, depth), bf16),
             pltpu.VMEM((near * BLOCK, depth), bf16),
             pltpu.VMEM((near * BLOCK, ff), bf16),
-            pltpu.VMEM((tok_rows, depth), bf16),
-            dma((1,)), dma((3,)), dma((2, depth // 2 // 512)),
-            dma((2, n)), dma((2, n)), dma((2, near)), dma((2, near)),
-            dma((2,)), dma((2,)), dma((n,)), dma((n,)),
+            dma((2,)), dma((3,)), dma((13,)), dma((13,)),
         ],
         compiler_params=pltpu.CompilerParams(
             collective_id=1, has_side_effects=True, vmem_limit_bytes=56 * 1024 * 1024
@@ -663,7 +674,7 @@
         return dispatch(*whole, pairs, eps)
     result, flag = spilling(*whole, pairs, eps)
     return lax.cond(
-        flag[0, 127] > 0,
+        flag[0, 0] > 0,
         lambda: dispatch(*whole, pairs, eps),
         lambda: result,
     )

time: 130 us -> 125 us (0.962)
  Pallas kernels: 127 us -> 123 us
    pallas_call x1, Pallas kernels: 127 us -> 123 us  [spilling(): pl.pallas_call(functools.partial(near_ffn, pairs, eps, spill), out_shape=...]
where the time goes in v2:
time: 125 us
  Pallas kernels  123 us (98%)
  local copies, waits for them, and re-layouts  1.33 us (1%)
    pallas_call x1, Pallas kernels, spilling(): pl.pallas_call(functools.partial(near_ffn, pairs, eps, spill), out_shape=...  123 us

profile of v2, /device:TPU:0, one launch (start us, length us, event | category | flops | bytes accessed | tf_op | source)
XLA Modules:
  0.0 124.7 jit_solution(15485086422801095072)
XLA Ops:
  0.0 0.0 copy-start
  0.0 0.0 copy-start.2
  0.0 122.7 %near_ffn.1 = (bf16[256,4096]{1,0:T(8,128)(2,1)S(1)}, f32[1,1]{1,0:T(1,128)}) custom-call(s32[1,256]{1,0:T(1,128)} %bitcast.9, bf16[256,4096]{1,0:T(8,128)(2,1)} %tok_hbm.1, bf16[1,4096,768]{2,1,0:T(8,128)(2,1)} %gate_hbm.1, bf16[1,4096,768]{2,1,0:T(8,128)(2,1)} %up_hbm.1, bf16[1,768,4096]{2,1,0:T(8,128)(2,1)} %down_hbm.1), custom_call_target="tpu_custom_call" | custom-call | tf_op jit(solution)/shard_map/near_ffn/pallas_call | solution.py:619
  123.3 0.0 copy-done
  123.3 0.0 copy-done.2
  123.3 1.3 %copy.15 = bf16[256,4096]{1,0:T(8,128)(2,1)} copy(bf16[256,4096]{1,0:T(8,128)(2,1)S(1)} %get-tuple-element.33) | data formatting | bytes 4194304
  (1 shorter events, 0.0 us)
Async XLA Ops:
  0.0 123.3 %copy-start = (bf16[256,4096]{1,0:T(8,128)(2,1)S(1)}, bf16[256,4096]{1,0:T(8,128)(2,1)}, u32[]{:S(2)}) copy-start(bf16[256,4096]{1,0:T(8,128)(2,1)} %tok_hbm.1) | copy-start | bytes 6291460
  0.0 123.3 %copy-start.2 = (s32[256,1]{0,1:T(1,128)S(1)}, s32[256,1]{0,1:T(1,128)}, u32[]{:S(2)}) copy-start(s32[256,1]{0,1:T(1,128)} %param.8) | copy-start | bytes 3076

commit v3 on v2

--- a/solution.py
+++ b/solution.py
@@ -297,16 +297,20 @@
 
 
 def near_ffn(
-    pairs, eps, spill, keys_hbm, tok_hbm, gate_hbm, up_hbm, down_hbm, total, flag_ref,
+    pairs, eps, spill, keys_hbm, tok_hbm, gate_hbm, up_hbm, down_hbm, total, flag_hbm,
     tok, send_b, recv_b, res_b, ret_b, send_x, recv_x, res_x, ret_x, send_s, recv_s, res_s, ret_s,
-    keys_ref, note, notes, gate, up, down, rows_x, hidden,
+    keys_ref, note, opinion, verdict, notes, gate, up, down, rows_x, hidden,
     load_sem, w_sem, ssem, rsem,
 ):
     n = pairs * eps
     near = n // 2
     line = eps // 2
     pair, ep = lax.axis_index("pair"), lax.axis_index("ep")
-    side, spot = ep // line, ep % line
+    rows_y = line // 2
+    quarter = near // 2
+    side = ep // line
+    spot = lax.rem(ep % line + rows_y * (1 - side), line)
+    outer, row_y = spot // rows_y, spot % rows_y
     tok_rows, depth = tok.shape
     mid = depth // 2
     ff = hidden.shape[1]
@@ -316,10 +320,13 @@
     wide = 512
 
     def peer(k, sign):
-        j = k % near + 1
-        p = lax.rem(pair + pairs + sign * (j // line % pairs), pairs)
-        s = lax.rem(spot + line + sign * (j % line), line)
-        return p, lax.rem(side + 1 - k // near, 2) * line + s
+        i = k % near
+        m = (i % quarter + 1) % quarter
+        p = lax.rem(pair + pairs + sign * (m % pairs), pairs)
+        y = lax.rem(row_y + rows_y + sign * (m // pairs), rows_y)
+        there = lax.rem(side + 1 - k // near, 2)
+        plane = lax.rem(outer + 1 - i // quarter + 1 - there, 2)
+        return p, there * line + plane * rows_y + y
 
     key_load = pltpu.make_async_copy(keys_hbm, keys_ref, load_sem.at[0])
     key_load.start()
@@ -336,61 +343,54 @@
         for i, (src, dst) in enumerate(((gate_hbm, gate), (up_hbm, up), (down_hbm, down)))
     ]
 
-    half = near // 2
     groups = {
-        "far_a": (send_b, recv_b, 0, half),
-        "far_b": (send_b, recv_b, half, near),
+        "far": (send_b, recv_b, 0, quarter),
+        "far_too": (send_b, recv_b, quarter, near),
         "close": (send_b, recv_b, near, n - 1),
         "extra": (send_x, recv_x, 0, near - 1),
         "spill": (send_s, recv_s, 0, spill),
-        "back_far_a": (res_b, ret_b, 0, half),
-        "back_far_b": (res_b, ret_b, half, near),
+        "back_far": (res_b, ret_b, 0, quarter),
+        "back_far_too": (res_b, ret_b, quarter, near),
         "back_close": (res_b, ret_b, near, n - 1),
         "back_extra": (res_x, ret_x, 0, near - 1),
         "back_spill": (res_s, ret_s, 0, spill),
     }
     ports = {name: i for i, name in enumerate(groups)}
 
-    def remote(name, src, dst, to, part=0):
-        at = ports[name] + part
+    def remote(at, src, dst, to):
         return pltpu.make_async_remote_copy(
             src_ref=src, dst_ref=dst, send_sem=ssem.at[at], recv_sem=rsem.at[at],
             device_id=to, device_id_type=MESH,
         )
 
-    mirror = (pair, lax.rem(side + 1, 2) * line + spot)
-
-    def go(name):
+    mirror = peer(near - 1, 1)
+
+    def go(name, turn=0):
         src, dst, low, high = groups[name]
         if src.shape[0] == spill:
-            remote(name, src, dst, mirror).start()
+            remote(ports[name], src, dst, mirror).start()
             return
         sign = -1 if name[:4] == "back" else 1
         skip = near if src.shape[0] == near else 0
 
-        @pl.loop(low, high)
-        def _(k):
-            remote(name, src.at[k], dst.at[k], peer(k + skip, sign)).start()
-
-    def group(name):
+        @pl.loop(0, high - low)
+        def _(i):
+            k = low + i + turn * quarter
+            remote(ports[name] + turn, src.at[k], dst.at[k], peer(k + skip, sign)).start()
+
+    def group(name, turn=0):
         src, dst, low, high = groups[name]
-        part = pl.ds(low, high - low)
-        return remote(name, src.at[part], dst.at[part], mirror)
-
+        part = pl.ds(low + turn * quarter, high - low)
+        return remote(ports[name] + turn, src.at[part], dst.at[part], mirror)
+
+    inner = 1 - outer
     last = len(groups)
-
-    def tell(k, part):
-        return pltpu.make_async_remote_copy(
-            src_ref=note, dst_ref=notes.at[k], send_sem=ssem.at[last + part],
-            recv_sem=rsem.at[last + part], device_id=peer(k, 1), device_id_type=MESH,
-        )
-
-    def told(low, high, part):
-        some = notes.at[pl.ds(low, high - low)]
-        return pltpu.make_async_remote_copy(
-            src_ref=some, dst_ref=some, send_sem=ssem.at[last + part],
-            recv_sem=rsem.at[last + part], device_id=mirror, device_id_type=MESH,
-        )
+    tell = remote(last, note, notes.at[near], mirror)
+
+    def vote(k):
+        return remote(last + 1, opinion, notes.at[k], peer(k + near, 1))
+
+    votes = remote(last + 1, notes.at[pl.ds(0, near - 1)], notes.at[pl.ds(0, near - 1)], mirror)
 
     def iota(shape, axis):
         return lax.broadcasted_iota(i32, shape, axis)
@@ -462,7 +462,7 @@
     excess = jnp.where(excess, 1.0, 0.0)
     note[...] = jnp.where(iota((1, 128), 1) == 127, excess, codes)
 
-    tell(near - 1, 0).start()
+    tell.start()
     far_hot = one_hot(far_key == iota((near * BLOCK, tok_rows), 0))
 
     @pl.loop(0, mid // wide)
@@ -470,9 +470,6 @@
         left = dot(far_hot, tok[:, split(0, c)])
         right = dot(far_hot, tok[:, split(mid, c)])
         send_b[pl.ds(0, near), :, split(0, c)] = weave(left, right, near)
-
-    go("far_a")
-    go("far_b")
 
     close_hot = one_hot(close_key == iota((2 * near * BLOCK, tok_rows), 0))
 
@@ -484,13 +481,18 @@
         send_b[pl.ds(near, near), :, split(0, c)] = weave(left[:body], right[:body], near)
         send_x[:, :, split(0, c)] = weave(left[body:], right[body:], near)
 
+    @pl.when(inner == 1)
+    def _():
+        go("far", inner)
+        go("far", outer)
+
     go("close")
 
     recv_b[n - 1] = send_b[n - 1]
 
-    tell(near - 1, 0).wait_recv()
+    tell.wait_recv()
     group("spill").wait_recv()
-    code = notes[near - 1]
+    code = notes[near]
     depth_s = spill * TILE
     placed = code[:, :depth_s].astype(i32) - 1
     place_hot = one_hot(placed == iota((near * TILE, depth_s), 0))
@@ -502,15 +504,19 @@
         send_x[:, :, split(0, c)] = (mine + moved).astype(bf16).reshape(near, TILE, wide)
 
     go("extra")
+
+    @pl.when(outer == 1)
+    def _():
+        go("far", inner)
+        go("far", outer)
+
     recv_x[near - 1] = send_x[near - 1]
+
+    opinion[...] = jnp.maximum(note[...], code)
 
     @pl.loop(0, near - 1)
     def _(k):
-        tell(k, 1).start()
-
-    @pl.loop(near, n - 1)
-    def _(k):
-        tell(k, 2).start()
+        vote(k).start()
 
     diagonal = iota((depth_s, 128), 0) == iota((depth_s, 128), 1)
     wanted = jnp.sum(jnp.where(diagonal, code, 0.0), axis=1, keepdims=True).astype(i32) - 1
@@ -560,22 +566,25 @@
     ffn(recv_b, res_b, near, near)
     go("back_close")
     ret_b[n - 1] = res_b[n - 1]
-    group("far_a").wait_recv()
-    ffn(recv_b, res_b, 0, half)
-    go("back_far_a")
     group("extra").wait_recv()
     ffn(recv_x, res_x, 0, near)
     go("back_extra")
     ret_x[near - 1] = res_x[near - 1]
-    group("far_b").wait_recv()
-    ffn(recv_b, res_b, half, half)
-    go("back_far_b")
-
-    for name in ("spill", "far_a", "far_b", "close", "extra"):
+    for turn in (inner, outer):
+        group("far", turn).wait_recv()
+        ffn(recv_b, res_b, turn * quarter, quarter)
+        go("back_far", turn)
+
+    for name in ("spill", "far", "far_too", "close", "extra"):
         group(name).wait_send()
-    tell(near - 1, 0).wait_send()
-    told(0, near - 1, 1).wait_send()
-    told(near, n - 1, 2).wait_send()
+    tell.wait_send()
+    votes.wait_send()
+    votes.wait_recv()
+    worst = jnp.maximum(jnp.max(notes[pl.ds(0, near - 1)], axis=0), opinion[...])
+    worst = jnp.where(iota((1, 128), 1) == 127, worst, 0.0)
+    verdict[...] = jnp.max(worst, axis=1, keepdims=True)
+    report = pltpu.make_async_copy(verdict, flag_hbm, load_sem.at[0])
+    report.start()
     group("back_extra").wait_recv()
 
     @pl.loop(0, mid // wide)
@@ -587,19 +596,23 @@
     unpack(col_x, ret_x, 0, near, True)
     group("back_close").wait_recv()
     unpack(col_b, ret_b, near, near, False)
-    told(0, near - 1, 1).wait_recv()
-    told(near, n - 1, 2).wait_recv()
-    notes[n - 1] = note[...]
-    worst = jnp.where(iota((1, 128), 1) == 127, jnp.max(notes[...], axis=0), 0.0)
-    flag_ref[0, 0] = jnp.max(worst)
-    group("back_far_a").wait_recv()
-    unpack(col_b, ret_b, 0, half, False)
-    group("back_far_b").wait_recv()
-    unpack(col_b, ret_b, half, half, False)
-    group("back_spill").wait_recv()
-    unpack(col_s, ret_s, 0, spill, False)
-    for name in ("back_close", "back_far_a", "back_extra", "back_far_b", "back_spill"):
+    def far(turn):
+        group("back_far", turn).wait_recv()
+        unpack(col_b, ret_b, turn * quarter, quarter, False)
+
+    def relayed(when):
+        @pl.when(outer == when)
+        def _():
+            group("back_spill").wait_recv()
+            unpack(col_s, ret_s, 0, spill, False)
+
+    far(inner)
+    relayed(1)
+    far(outer)
+    relayed(0)
+    for name in ("back_close", "back_far", "back_far_too", "back_extra", "back_spill"):
         group(name).wait_send()
+    report.wait()
 
 
 def spilling(tokens, routed, w_gate, w_up, w_down, pairs, eps):
@@ -623,7 +636,7 @@
             jax.ShapeDtypeStruct((1, 1), f32),
         ],
         in_specs=[hbm, hbm, hbm, hbm, hbm],
-        out_specs=[vmem, pl.BlockSpec(memory_space=pltpu.SMEM)],
+        out_specs=[vmem, hbm],
         scratch_shapes=[
             pltpu.VMEM((tok_rows, depth), bf16),
             *[blocks(n)] * 4,
@@ -631,13 +644,15 @@
             *[blocks(spill)] * 4,
             pltpu.VMEM((1, tok_rows), jnp.int32),
             pltpu.VMEM((1, 128), f32),
-            pltpu.VMEM((n, 1, 128), f32),
+            pltpu.VMEM((1, 128), f32),
+            pltpu.VMEM((1, 1), f32),
+            pltpu.VMEM((near + 1, 1, 128), f32),
             pltpu.VMEM((depth, ff), bf16),
             pltpu.VMEM((depth, ff), bf16),
             pltpu.VMEM((ff, depth), bf16),
             pltpu.VMEM((near * BLOCK, depth), bf16),
             pltpu.VMEM((near * BLOCK, ff), bf16),
-            dma((2,)), dma((3,)), dma((13,)), dma((13,)),
+            dma((2,)), dma((3,)), dma((12,)), dma((12,)),
         ],
         compiler_params=pltpu.CompilerParams(
             collective_id=1, has_side_effects=True, vmem_limit_bytes=56 * 1024 * 1024
@@ -669,7 +684,7 @@
     tok_rows, depth = tokens.shape
     routed = expert_of[:, 0]
     whole = (tokens, routed, w_gate, w_up, w_down)
-    even = tok_rows == BLOCK * experts and eps % 2 == 0 and experts % (2 * GROUP) == 0
+    even = tok_rows == BLOCK * experts and eps % 4 == 0 and experts % (2 * GROUP) == 0
     if not (even and depth % 1024 == 0 and w_gate.shape[2] % 256 == 0):
         return dispatch(*whole, pairs, eps)
     result, flag = spilling(*whole, pairs, eps)

time: 125 us -> 122 us (0.976)
  Pallas kernels: 123 us -> 120 us
    pallas_call x1, Pallas kernels: 123 us -> 120 us  [spilling(): pl.pallas_call(functools.partial(near_ffn, pairs, eps, spill), out_shape=...]
where the time goes in v3:
time: 122 us
  Pallas kernels  120 us (98%)
  local copies, waits for them, and re-layouts  1.33 us (1%)
    pallas_call x1, Pallas kernels, spilling(): pl.pallas_call(functools.partial(near_ffn, pairs, eps, spill), out_shape=...  120 us

profile of v3, /device:TPU:0, one launch (start us, length us, event | category | flops | bytes accessed | tf_op | source)
XLA Modules:
  0.0 122.3 jit_solution(16869153252541729004)
XLA Ops:
  0.0 0.0 copy-start
  0.0 0.0 copy-start.2
  0.0 120.4 %near_ffn.1 = (bf16[256,4096]{1,0:T(8,128)(2,1)S(1)}, f32[1,1]{1,0:T(1,128)}) custom-call(s32[1,256]{1,0:T(1,128)} %bitcast.9, bf16[256,4096]{1,0:T(8,128)(2,1)} %tok_hbm.1, bf16[1,4096,768]{2,1,0:T(8,128)(2,1)} %gate_hbm.1, bf16[1,4096,768]{2,1,0:T(8,128)(2,1)} %up_hbm.1, bf16[1,768,4096]{2,1,0:T(8,128)(2,1)} %down_hbm.1), custom_call_target="tpu_custom_call" | custom-call | tf_op jit(solution)/shard_map/near_ffn/pallas_call | solution.py:632
  121.0 0.0 copy-done
  121.0 0.0 copy-done.2
  121.0 1.3 %copy.15 = bf16[256,4096]{1,0:T(8,128)(2,1)} copy(bf16[256,4096]{1,0:T(8,128)(2,1)S(1)} %get-tuple-element.33) | data formatting | bytes 4194304
  (1 shorter events, 0.0 us)
Async XLA Ops:
  0.0 121.0 %copy-start = (bf16[256,4096]{1,0:T(8,128)(2,1)S(1)}, bf16[256,4096]{1,0:T(8,128)(2,1)}, u32[]{:S(2)}) copy-start(bf16[256,4096]{1,0:T(8,128)(2,1)} %tok_hbm.1) | copy-start | bytes 6291460
  0.0 121.0 %copy-start.2 = (s32[256,1]{0,1:T(1,128)S(1)}, s32[256,1]{0,1:T(1,128)}, u32[]{:S(2)}) copy-start(s32[256,1]{0,1:T(1,128)} %param.8) | copy-start | bytes 3076

commit v4 on v3

--- a/solution.py
+++ b/solution.py
@@ -328,15 +328,14 @@
         plane = lax.rem(outer + 1 - i // quarter + 1 - there, 2)
         return p, there * line + plane * rows_y + y
 
+    barrier = pltpu.get_barrier_semaphore()
+    for k in range(n - 1):
+        pl.semaphore_signal(barrier, inc=1, device_id=peer(k, 1), device_id_type=MESH)
+
     key_load = pltpu.make_async_copy(keys_hbm, keys_ref, load_sem.at[0])
     key_load.start()
     tok_load = pltpu.make_async_copy(tok_hbm, tok, load_sem.at[1])
     tok_load.start()
-    barrier = pltpu.get_barrier_semaphore()
-
-    @pl.loop(0, n - 1)
-    def _(k):
-        pl.semaphore_signal(barrier, inc=1, device_id=peer(k, 1), device_id_type=MESH)
 
     loads = [
         pltpu.make_async_copy(src.at[0], dst, w_sem.at[i])
@@ -570,7 +569,7 @@
     ffn(recv_x, res_x, 0, near)
     go("back_extra")
     ret_x[near - 1] = res_x[near - 1]
-    for turn in (inner, outer):
+    for turn in (1, 0):
         group("far", turn).wait_recv()
         ffn(recv_b, res_b, turn * quarter, quarter)
         go("back_far", turn)
@@ -606,9 +605,9 @@
             group("back_spill").wait_recv()
             unpack(col_s, ret_s, 0, spill, False)
 
-    far(inner)
     relayed(1)
-    far(outer)
+    far(1)
+    far(0)
     relayed(0)
     for name in ("back_close", "back_far", "back_far_too", "back_extra", "back_spill"):
         group(name).wait_send()

time: 122 us -> 120 us (0.984); the launches traced: 122 us -> 118 us
  Pallas kernels: 120 us -> 116 us
    pallas_call x1, Pallas kernels: 120 us -> 116 us  [spilling(): pl.pallas_call(functools.partial(near_ffn, pairs, eps, spill), out_shape=...]
where the time goes in v4:
time: 120 us; the launch traced here: 118 us
  Pallas kernels  116 us (97%)
  local copies, waits for them, and re-layouts  1.33 us (1%)
    pallas_call x1, Pallas kernels, spilling(): pl.pallas_call(functools.partial(near_ffn, pairs, eps, spill), out_shape=...  116 us

profile of v4, /device:TPU:0, one launch (start us, length us, event | category | flops | bytes accessed | tf_op | source)
XLA Modules:
  0.0 118.4 jit_solution(11503173593966250566)
XLA Ops:
  0.0 0.0 copy-start
  0.0 0.0 copy-start.2
  0.0 116.5 %near_ffn.1 = (bf16[256,4096]{1,0:T(8,128)(2,1)S(1)}, f32[1,1]{1,0:T(1,128)}) custom-call(s32[1,256]{1,0:T(1,128)} %bitcast.9, bf16[256,4096]{1,0:T(8,128)(2,1)} %tok_hbm.1, bf16[1,4096,768]{2,1,0:T(8,128)(2,1)} %gate_hbm.1, bf16[1,4096,768]{2,1,0:T(8,128)(2,1)} %up_hbm.1, bf16[1,768,4096]{2,1,0:T(8,128)(2,1)} %down_hbm.1), custom_call_target="tpu_custom_call" | custom-call | tf_op jit(solution)/shard_map/near_ffn/pallas_call | solution.py:631
  117.0 0.0 copy-done
  117.0 0.0 copy-done.2
  117.1 1.3 %copy.15 = bf16[256,4096]{1,0:T(8,128)(2,1)} copy(bf16[256,4096]{1,0:T(8,128)(2,1)S(1)} %get-tuple-element.33) | data formatting | bytes 4194304
  (1 shorter events, 0.0 us)
Async XLA Ops:
  0.0 117.0 %copy-start = (bf16[256,4096]{1,0:T(8,128)(2,1)S(1)}, bf16[256,4096]{1,0:T(8,128)(2,1)}, u32[]{:S(2)}) copy-start(bf16[256,4096]{1,0:T(8,128)(2,1)} %tok_hbm.1) | copy-start | bytes 6291460
  0.0 117.0 %copy-start.2 = (s32[256,1]{0,1:T(1,128)S(1)}, s32[256,1]{0,1:T(1,128)}, u32[]{:S(2)}) copy-start(s32[256,1]{0,1:T(1,128)} %param.8) | copy-start | bytes 3076

commit v5 on v4

--- a/solution.py
+++ b/solution.py
@@ -384,6 +384,28 @@
 
     inner = 1 - outer
     last = len(groups)
+    late = {"back_far": last + 2, "back_spill": last + 3}
+
+    def lanes(j):
+        return pl.ds(j * (mid // 2), mid // 2)
+
+    def go_half(name, j):
+        src, dst, low, high = groups[name]
+        at = late[name] if j else ports[name]
+        if src.shape[0] == spill:
+            remote(at, src.at[:, :, lanes(j)], dst.at[:, :, lanes(j)], mirror).start()
+            return
+
+        @pl.loop(low, high)
+        def _(k):
+            remote(at, src.at[k, :, lanes(j)], dst.at[k, :, lanes(j)], peer(k, -1)).start()
+
+    def half_group(name, j):
+        src, dst, low, high = groups[name]
+        part = pl.ds(low, high - low)
+        at = late[name] if j else ports[name]
+        return remote(at, src.at[part, :, lanes(j)], dst.at[part, :, lanes(j)], mirror)
+
     tell = remote(last, note, notes.at[near], mirror)
 
     def vote(k):
@@ -548,13 +570,15 @@
             right = dot(hidden[:rows, :], down[:, split(mid, c)])
             result[pl.ds(base, count), :, split(0, c)] = weave(left, right, count)
 
-    def unpack(col, returned, base, count, start):
+    def unpack(col, returned, base, count, start, part=None):
         depth_k = count * TILE
         at = iota((tok_rows, depth_k), 1) + base * TILE
         left_hot = one_hot(col == at)
         right_hot = one_hot(col + BLOCK == at)
-
-        @pl.loop(0, mid // wide)
+        chunks = mid // wide
+        low, high = (0, chunks) if part is None else (part * chunks // 2, (part + 1) * chunks // 2)
+
+        @pl.loop(low, high)
         def _(c):
             piece = returned[pl.ds(base, count), :, split(0, c)].reshape(depth_k, wide)
             for hot, half in ((left_hot, 0), (right_hot, mid)):
@@ -572,7 +596,11 @@
     for turn in (1, 0):
         group("far", turn).wait_recv()
         ffn(recv_b, res_b, turn * quarter, quarter)
-        go("back_far", turn)
+        if turn:
+            go("back_far", turn)
+        else:
+            go_half("back_far", 0)
+            go_half("back_far", 1)
 
     for name in ("spill", "far", "far_too", "close", "extra"):
         group(name).wait_send()
@@ -591,26 +619,30 @@
         piece = ret_x[:, :, split(0, c)].reshape(near * TILE, wide)
         res_s[:, :, split(0, c)] = dot(fetch_hot, piece).astype(bf16).reshape(spill, TILE, wide)
 
-    go("back_spill")
+    go_half("back_spill", 0)
+    go_half("back_spill", 1)
     unpack(col_x, ret_x, 0, near, True)
     group("back_close").wait_recv()
     unpack(col_b, ret_b, near, near, False)
-    def far(turn):
-        group("back_far", turn).wait_recv()
-        unpack(col_b, ret_b, turn * quarter, quarter, False)
-
     def relayed(when):
         @pl.when(outer == when)
         def _():
-            group("back_spill").wait_recv()
-            unpack(col_s, ret_s, 0, spill, False)
+            for j in range(2):
+                half_group("back_spill", j).wait_recv()
+                unpack(col_s, ret_s, 0, spill, False, j)
 
     relayed(1)
-    far(1)
-    far(0)
+    group("back_far", 1).wait_recv()
+    unpack(col_b, ret_b, quarter, quarter, False)
+    for j in range(2):
+        half_group("back_far", j).wait_recv()
+        unpack(col_b, ret_b, 0, quarter, False, j)
     relayed(0)
-    for name in ("back_close", "back_far", "back_far_too", "back_extra", "back_spill"):
+    for name in ("back_close", "back_far_too", "back_extra"):
         group(name).wait_send()
+    for j in range(2):
+        half_group("back_far", j).wait_send()
+        half_group("back_spill", j).wait_send()
     report.wait()
 
 
@@ -651,7 +683,7 @@
             pltpu.VMEM((ff, depth), bf16),
             pltpu.VMEM((near * BLOCK, depth), bf16),
             pltpu.VMEM((near * BLOCK, ff), bf16),
-            dma((2,)), dma((3,)), dma((12,)), dma((12,)),
+            dma((2,)), dma((3,)), dma((14,)), dma((14,)),
         ],
         compiler_params=pltpu.CompilerParams(
             collective_id=1, has_side_effects=True, vmem_limit_bytes=56 * 1024 * 1024

time: 120 us -> 120 us (level)
  no operation moved by 1% of the time
where the time goes in v5:
time: 120 us; the launch traced here: 118 us
  Pallas kernels  116 us (97%)
  local copies, waits for them, and re-layouts  1.33 us (1%)
    pallas_call x1, Pallas kernels, spilling(): pl.pallas_call(functools.partial(near_ffn, pairs, eps, spill), out_shape=...  116 us

profile of v5, /device:TPU:0, one launch (start us, length us, event | category | flops | bytes accessed | tf_op | source)
XLA Modules:
  0.0 118.0 jit_solution(8732508503115223265)
XLA Ops:
  0.0 0.0 copy-start
  0.0 0.0 copy-start.2
  0.0 115.9 %near_ffn.1 = (bf16[256,4096]{1,0:T(8,128)(2,1)S(1)}, f32[1,1]{1,0:T(1,128)}) custom-call(s32[1,256]{1,0:T(1,128)} %bitcast.9, bf16[256,4096]{1,0:T(8,128)(2,1)} %tok_hbm.1, bf16[1,4096,768]{2,1,0:T(8,128)(2,1)} %gate_hbm.1, bf16[1,4096,768]{2,1,0:T(8,128)(2,1)} %up_hbm.1, bf16[1,768,4096]{2,1,0:T(8,128)(2,1)} %down_hbm.1), custom_call_target="tpu_custom_call" | custom-call | tf_op jit(solution)/shard_map/near_ffn/pallas_call | solution.py:663
  116.5 0.0 copy-done
  116.5 0.0 copy-done.2
  116.5 0.2 conditional.1
  116.7 1.3 %copy.15 = bf16[256,4096]{1,0:T(8,128)(2,1)} copy(bf16[256,4096]{1,0:T(8,128)(2,1)S(1)} %get-tuple-element.33) | data formatting | bytes 4194304
Async XLA Ops:
  0.0 116.5 %copy-start = (bf16[256,4096]{1,0:T(8,128)(2,1)S(1)}, bf16[256,4096]{1,0:T(8,128)(2,1)}, u32[]{:S(2)}) copy-start(bf16[256,4096]{1,0:T(8,128)(2,1)} %tok_hbm.1) | copy-start | bytes 6291460
  0.0 116.5 %copy-start.2 = (s32[256,1]{0,1:T(1,128)S(1)}, s32[256,1]{0,1:T(1,128)}, u32[]{:S(2)}) copy-start(s32[256,1]{0,1:T(1,128)} %param.8) | copy-start | bytes 3076

commit v6 on v5

--- a/solution.py
+++ b/solution.py
@@ -505,9 +505,12 @@
     @pl.when(inner == 1)
     def _():
         go("far", inner)
+
+    go("close")
+
+    @pl.when(inner == 1)
+    def _():
         go("far", outer)
-
-    go("close")
 
     recv_b[n - 1] = send_b[n - 1]
 

time: 120 us -> 120 us (level)
  no operation moved by 1% of the time
where the time goes in v6:
time: 120 us; the launch traced here: 118 us
  Pallas kernels  116 us (97%)
  local copies, waits for them, and re-layouts  1.33 us (1%)
    pallas_call x1, Pallas kernels, spilling(): pl.pallas_call(functools.partial(near_ffn, pairs, eps, spill), out_shape=...  116 us

profile of v6, /device:TPU:0, one launch (start us, length us, event | category | flops | bytes accessed | tf_op | source)
XLA Modules:
  0.0 118.2 jit_solution(16331929064307478648)
XLA Ops:
  0.0 0.0 copy-start
  0.0 0.0 copy-start.2
  0.0 116.1 %near_ffn.1 = (bf16[256,4096]{1,0:T(8,128)(2,1)S(1)}, f32[1,1]{1,0:T(1,128)}) custom-call(s32[1,256]{1,0:T(1,128)} %bitcast.9, bf16[256,4096]{1,0:T(8,128)(2,1)} %tok_hbm.1, bf16[1,4096,768]{2,1,0:T(8,128)(2,1)} %gate_hbm.1, bf16[1,4096,768]{2,1,0:T(8,128)(2,1)} %up_hbm.1, bf16[1,768,4096]{2,1,0:T(8,128)(2,1)} %down_hbm.1), custom_call_target="tpu_custom_call" | custom-call | tf_op jit(solution)/shard_map/near_ffn/pallas_call | solution.py:666
  116.7 0.0 copy-done
  116.7 0.0 copy-done.2
  116.7 0.2 conditional.1
  116.9 1.3 %copy.15 = bf16[256,4096]{1,0:T(8,128)(2,1)} copy(bf16[256,4096]{1,0:T(8,128)(2,1)S(1)} %get-tuple-element.33) | data formatting | bytes 4194304
Async XLA Ops:
  0.0 116.7 %copy-start = (bf16[256,4096]{1,0:T(8,128)(2,1)S(1)}, bf16[256,4096]{1,0:T(8,128)(2,1)}, u32[]{:S(2)}) copy-start(bf16[256,4096]{1,0:T(8,128)(2,1)} %tok_hbm.1) | copy-start | bytes 6291460
  0.0 116.7 %copy-start.2 = (s32[256,1]{0,1:T(1,128)S(1)}, s32[256,1]{0,1:T(1,128)}, u32[]{:S(2)}) copy-start(s32[256,1]{0,1:T(1,128)} %param.8) | copy-start | bytes 3076
